TPU v7x, 32 devices: a whole 2x2x4 slice. The times are simulated.
32 devices in a mesh: grp: 4 (over x, core), mem: 8 (over z, y).
Axes of the slice: x: 2, y: 2, z: 4, core: 2. Of those that a mesh axis runs over, the one named last changes fastest.
Arguments:
- source_pts: float32 [64, 8192], P(None, ('grp', 'mem')), may hold values from -30 to 30
- target_pts: float32 [64, 8192], P(None, ('grp', 'mem')), may hold values from -30 to 30
- source_pot: float32 [8192], P(('grp', 'mem')), may hold values from -8 to 520
- target_pot: float32 [8192], P(('grp', 'mem')), may hold values from -8 to 520
- source_logw: float32 [8192], P(('grp', 'mem')), may hold values from -1 to 4
- target_logw: float32 [8192], P(('grp', 'mem')), may hold values from -1 to 4
Outputs:
- source_new: float32 [8192], P(('grp', 'mem'))
- target_new: float32 [8192], P(('grp', 'mem'))
All inputs are finite; a program needn't handle non-finite values.
Results may differ from a plain program's by a relative error of at most 0.0001.
Values sent between devices are 32-bit elements; how exact they have to be, the bound alone decides.
A program may use at most 64 MiB of HBM per device.

v0:
```python
import math
import jax
import jax.numpy as jnp
from jax import lax
from jax.sharding import PartitionSpec as P

epsilon = 4.0
floor_value = -1e30


def sweep(carry, points, squares, row_term, moving, offset):
    count = moving.shape[1]
    limit = 128
    width = math.gcd(count, limit)

    def block(index, state):
        row_max, row_sum, col_max, col_sum = state
        begin = index * width
        cols = lax.dynamic_slice_in_dim(moving, begin, width, 1)
        ycols = cols[:-1]
        cvals = cols[-1]
        ysq = 0.5 * jnp.sum(ycols * ycols, 0)
        cross = lax.dot_general(
            points,
            ycols,
            (((0,), (0,)), ((), ())),
            precision=lax.Precision.HIGHEST,
            preferred_element_type=jnp.float32,
        )
        half = (squares[:, None] + ysq[None, :] - cross) / epsilon
        scores = cvals[None, :] - half
        new_row = jnp.maximum(row_max, jnp.max(scores, 1))
        row_sum = row_sum * jnp.exp(row_max - new_row) + jnp.sum(
            jnp.exp(scores - new_row[:, None]), 1
        )
        others = row_term[:, None] - half
        place = offset + begin
        old_max = lax.dynamic_slice_in_dim(col_max, place, width, 0)
        old_sum = lax.dynamic_slice_in_dim(col_sum, place, width, 0)
        new_col = jnp.maximum(old_max, jnp.max(others, 0))
        new_sum = old_sum * jnp.exp(old_max - new_col) + jnp.sum(
            jnp.exp(others - new_col[None, :]), 0
        )
        col_max = lax.dynamic_update_slice_in_dim(col_max, new_col, place, 0)
        col_sum = lax.dynamic_update_slice_in_dim(col_sum, new_sum, place, 0)
        return (new_row, row_sum, col_max, col_sum)

    return lax.fori_loop(0, count // width, block, carry)


def totals(source_logw, target_logw):
    peaks = lax.pmax((jnp.max(source_logw), jnp.max(target_logw)), ("grp", "mem"))
    masses = lax.psum(
        (jnp.sum(jnp.exp(source_logw - peaks[0])), jnp.sum(jnp.exp(target_logw - peaks[1]))),
        ("grp", "mem"),
    )
    return (peaks[0] + jnp.log(masses[0]), peaks[1] + jnp.log(masses[1]))


def local(source_pts, target_pts, source_pot, target_pot, source_logw, target_logw):
    members = lax.axis_size("mem")
    rows = source_pts.shape[1]
    outer = rows * members
    src_norm, tgt_norm = totals(source_logw, target_logw)
    row_term = source_logw - src_norm + source_pot / epsilon
    col_term = target_logw - tgt_norm + target_pot / epsilon
    moving = jnp.concatenate([target_pts, col_term[None, :]], 0)
    standing = jnp.concatenate([source_pts, row_term[None, :]], 0)
    row_block = lax.all_gather(standing, "mem", axis=1, tiled=True)
    col_block = lax.all_gather(moving, "grp", axis=1, tiled=True)
    block_pts = row_block[:-1]
    block_terms = row_block[-1]
    block_sq = 0.5 * jnp.sum(block_pts * block_pts, 0)
    span = col_block.shape[1]
    carry = (
        jnp.full((outer,), floor_value, jnp.float32),
        jnp.zeros((outer,), jnp.float32),
        jnp.full((span,), floor_value, jnp.float32),
        jnp.zeros((span,), jnp.float32),
    )
    row_max, row_sum, col_max, col_sum = sweep(
        carry, block_pts, block_sq, block_terms, col_block, 0
    )
    rpeak = lax.pmax(row_max, "mem")
    own_rsum = lax.psum_scatter(
        row_sum * jnp.exp(row_max - rpeak), "mem", scatter_dimension=0, tiled=True
    )
    own_rmax = lax.dynamic_slice_in_dim(rpeak, lax.axis_index("mem") * rows, rows, 0)
    row_total = own_rmax + jnp.log(own_rsum)
    cpeak = lax.pmax(col_max, "grp")
    own_sum = lax.psum_scatter(
        col_sum * jnp.exp(col_max - cpeak), "grp", scatter_dimension=0, tiled=True
    )
    own_max = lax.dynamic_slice_in_dim(cpeak, lax.axis_index("grp") * rows, rows, 0)
    col_total = own_max + jnp.log(own_sum)
    row_hat = -epsilon * row_total
    col_hat = -epsilon * col_total
    return (0.5 * (source_pot + row_hat), 0.5 * (target_pot + col_hat))


def solution(mesh):
    return jax.shard_map(
        local,
        mesh=mesh,
        in_specs=(
            P(None, ("grp", "mem")),
            P(None, ("grp", "mem")),
            P(("grp", "mem")),
            P(("grp", "mem")),
            P(("grp", "mem")),
            P(("grp", "mem")),
        ),
        out_specs=(P(("grp", "mem")), P(("grp", "mem"))),
        check_vma=False,
    )
```

profile of v0, /device:TPU:0, one launch (start us, length us, event | category | flops | bytes accessed | tf_op | source)
XLA Modules:
  0.0 205.6 jit_solution(15678545301726195394)
XLA Ops:
  0.6 1.3 reduce_max.44
  2.5 42.2 %all-reduce.3 = (f32[]{:T(128)}, f32[]{:T(128)}) all-reduce(f32[]{:T(128)} %reduce_max.44, f32[]{:T(128)} %reduce_max.45), channel_id=1, replica_groups=mesh['grp'=4,'mem'=8] {'grp','mem'}, use_global_device_ids=true, to_apply=%region_1.0 | all-reduce | flops 2 | bytes 16 | tf_op jit(solution)/shard_map/pmax | solution.py:52
  44.8 0.7 copy-done.3
  45.4 2.0 exponential_reduce_fusion.2
  47.4 40.6 %all-reduce.2 = (f32[]{:T(128)}, f32[]{:T(128)}) all-reduce(f32[]{:T(128)} %get-tuple-element.225, f32[]{:T(128)} %get-tuple-element.224), channel_id=1, replica_groups=mesh['grp'=4,'mem'=8] {'grp','mem'}, use_global_device_ids=true, to_apply=%region_3.0 | all-reduce | flops 2 | bytes 16 | tf_op jit(solution)/shard_map/psum | solution.py:53
  89.3 0.8 pad_maximum_fusion.1
  90.2 31.4 %all_gather.7 = f32[65,2048]{1,0:T(8,128)S(1)} all-gather(f32[65,256]{1,0:T(8,128)S(1)} %pad_maximum_fusion.1), channel_id=1, replica_groups=mesh['grp'=4,'mem'=8] {'mem'}, dimensions={1}, use_global_device_ids=true | all-gather | bytes 599040 | tf_op jit(solution)/shard_map/all_gather | solution.py:69
  121.7 0.7 copy-done
  123.8 6.7 %all_gather.6 = f32[65,1024]{1,0:T(8,128)S(1)} all-gather(f32[65,256]{1,0:T(8,128)S(1)} %pad_maximum_fusion), channel_id=1, replica_groups=mesh['grp'=4,'mem'=8] {'grp'}, dimensions={1}, use_global_device_ids=true | all-gather | bytes 332800 | tf_op jit(solution)/shard_map/all_gather | solution.py:70
  130.5 0.7 slice-done
  131.2 18.0 %while.20 = (s32[]{:T(128)}, f32[2048]{0:T(1024)S(1)}, f32[2048]{0:T(1024)S(1)}, f32[1024]{0:T(1024)S(1)}, f32[1024]{0:T(1024)S(1)}, /*index=5*/f32[65,1024]{1,0...) while((s32[]{:T(128)}, f32[2048]{0:T(1024)S(1)}, ...), condition=%wide.region_15.0_spmd.clone, body=%wide.region_9.0_spmd.clone.sunk | while | flops 204761344 | bytes 2844898 | solution.py:48
  131.2 1.3 subtract_reduce_fusion.3
  133.5 1.3 subtract_reduce_fusion.3
  135.7 1.3 subtract_reduce_fusion.3
  138.0 1.3 subtract_reduce_fusion.3
  140.2 1.3 subtract_reduce_fusion.3
  142.5 1.3 subtract_reduce_fusion.3
  144.8 1.3 subtract_reduce_fusion.3
  147.0 1.3 subtract_reduce_fusion.3
  149.2 7.1 %pmax.31 = f32[1024]{0:T(1024)S(1)} all-reduce(f32[1024]{0:T(1024)S(1)} %get-tuple-element.161), channel_id=1, replica_groups=mesh['grp'=4,'mem'=8] {'grp'}, use_global_device_ids=true, to_apply=%region_18.0 | all-reduce | flops 1024 | bytes 8192 | tf_op jit(solution)/shard_map/pmax | solution.py:90
  156.3 6.0 %all-reduce.1 = f32[1024]{0:T(1024)S(1)} all-reduce(f32[1024]{0:T(1024)S(1)} %exponential_multiply_fusion.1), channel_id=3, replica_groups=mesh['grp'=4,'mem'=8] {'grp'}, use_global_device_ids=true, to_apply=%region_19.0.clone | all-reduce | flops 1024 | bytes 8192
  164.8 20.8 %pmax.30 = f32[2048]{0:T(1024)S(1)} all-reduce(f32[2048]{0:T(1024)S(1)} %get-tuple-element.159), channel_id=1, replica_groups=mesh['grp'=4,'mem'=8] {'mem'}, use_global_device_ids=true, to_apply=%region_16.0 | all-reduce | flops 2048 | bytes 16384 | tf_op jit(solution)/shard_map/pmax | solution.py:84
  185.7 17.4 %all-reduce = f32[2048]{0:T(1024)S(1)} all-reduce(f32[2048]{0:T(1024)S(1)} %exponential_multiply_fusion), channel_id=2, replica_groups=mesh['grp'=4,'mem'=8] {'mem'}, use_global_device_ids=true, to_apply=%region_17.0.clone | all-reduce | flops 2048 | bytes 16384
  205.0 0.7 fusion.11
  (118 shorter events, 10.9 us)
Async XLA Ops:
  0.6 1.3 copy-start.2
  44.8 0.7 copy-start.3
  88.6 0.7 copy-start.5
  121.6 0.8 copy-start
  121.6 2.1 %copy-start.1 = (f32[64,256]{1,0:T(8,128)S(1)}, f32[64,256]{1,0:T(8,128)}, u32[]{:S(2)}) copy-start(f32[64,256]{1,0:T(8,128)} %param.9) | copy-start | bytes 196612
  123.0 0.7 copy-start.4
  130.5 0.7 slice-start
  162.3 0.7 copy-start.7
  203.1 0.7 copy-start.6
where the time goes:
time: 206 us
  blocking collectives  172 us (83%)
  other arithmetic  13 us (6%)
  matrix products  10.4 us (5%)
  local copies, waits for them, and re-layouts  4.74 us (2%)
  between operations  4.67 us (2%)
    pmax x1, blocking collectives, totals(): lax.pmax((jnp.max(source_logw), jnp.max(target_logw)), ('grp', 'mem'))  42.2 us
    psum x1, blocking collectives, totals(): lax.psum((jnp.sum(jnp.exp(source_logw - peaks[0])), jnp.sum(jnp.exp(targe...  40.6 us
    all_gather x1, blocking collectives, local(): row_block = lax.all_gather(standing, 'mem', axis=1, tiled=True)  31.4 us
    unnamed x2, blocking collectives  23.4 us
    pmax x1, blocking collectives, local(): rpeak = lax.pmax(row_max, 'mem')  20.8 us
    dot_general x8, matrix products, block(): lax.dot_general(points, ycols, (((0,), (0,)), ((), ())), precision=lax.Pr...  10.4 us
    pmax x1, blocking collectives, local(): cpeak = lax.pmax(col_max, 'grp')  7.05 us
    all_gather x1, blocking collectives, local(): col_block = lax.all_gather(moving, 'grp', axis=1, tiled=True)  6.72 us

commit v1 on v0

--- a/solution.py
+++ b/solution.py
@@ -51,8 +51,11 @@
 def totals(source_logw, target_logw):
     peaks = lax.pmax((jnp.max(source_logw), jnp.max(target_logw)), ("grp", "mem"))
     masses = lax.psum(
-        (jnp.sum(jnp.exp(source_logw - peaks[0])), jnp.sum(jnp.exp(target_logw - peaks[1]))),
-        ("grp", "mem"),
+        lax.psum(
+            (jnp.sum(jnp.exp(source_logw - peaks[0])), jnp.sum(jnp.exp(target_logw - peaks[1]))),
+            "mem",
+        ),
+        "grp",
     )
     return (peaks[0] + jnp.log(masses[0]), peaks[1] + jnp.log(masses[1]))
 

time: 206 us -> 191 us (0.927)
  blocking collectives: 172 us -> 157 us
    psum x1, blocking collectives: 40.6 us -> 21.9 us  [totals(): lax.psum((jnp.sum(jnp.exp(source_logw - peaks[0])), jnp.sum(jnp.exp(targe...]
    psum x0 -> x1, blocking collectives: none -> 6.57 us  [totals(): lax.psum(lax.psum((jnp.sum(jnp.exp(source_logw - peaks[0])), jnp.sum(jnp....]
    pmax x1, blocking collectives: 20.8 us -> 17.5 us  [local(): rpeak = lax.pmax(row_max, 'mem')]
where the time goes in v1:
time: 191 us; the launch traced here: 190 us
  blocking collectives  157 us (82%)
  other arithmetic  13 us (7%)
  matrix products  10.4 us (5%)
  local copies, waits for them, and re-layouts  4.74 us (2%)
  between operations  4.67 us (2%)
    pmax x1, blocking collectives, totals(): lax.pmax((jnp.max(source_logw), jnp.max(target_logw)), ('grp', 'mem'))  42.2 us
    all_gather x1, blocking collectives, local(): row_block = lax.all_gather(standing, 'mem', axis=1, tiled=True)  31.4 us
    unnamed x2, blocking collectives  25 us
    psum x1, blocking collectives, totals(): lax.psum((jnp.sum(jnp.exp(source_logw - peaks[0])), jnp.sum(jnp.exp(targe...  21.9 us
    pmax x1, blocking collectives, local(): rpeak = lax.pmax(row_max, 'mem')  17.5 us
    dot_general x8, matrix products, block(): lax.dot_general(points, ycols, (((0,), (0,)), ((), ())), precision=lax.Pr...  10.4 us
    psum x1, blocking collectives, totals(): lax.psum(lax.psum((jnp.sum(jnp.exp(source_logw - peaks[0])), jnp.sum(jnp....  6.57 us
    pmax x1, blocking collectives, local(): cpeak = lax.pmax(col_max, 'grp')  6.2 us

profile of v1, /device:TPU:0, one launch (start us, length us, event | category | flops | bytes accessed | tf_op | source)
XLA Modules:
  0.0 190.0 jit_solution(2839522664484192782)
XLA Ops:
  0.6 1.3 reduce_max.44
  2.5 42.2 %all-reduce.2 = (f32[]{:T(128)}, f32[]{:T(128)}) all-reduce(f32[]{:T(128)} %reduce_max.44, f32[]{:T(128)} %reduce_max.45), channel_id=1, replica_groups=mesh['grp'=4,'mem'=8] {'grp','mem'}, use_global_device_ids=true, to_apply=%region_1.0 | all-reduce | flops 2 | bytes 16 | tf_op jit(solution)/shard_map/pmax | solution.py:52
  44.7 0.7 copy-done.3
  45.4 2.0 %exponential_reduce_fusion.2 = (f32[]{:T(128)}, f32[]{:T(128)}) fusion(f32[256]{0:T(256)S(1)} %copy-done.2, f32[]{:T(128)} %get-tuple-element.216, f32[256]{0:T(256)S(1)} %copy-done.3, f32[]{:T(128)} %get-tuple-element.215), kind=kLoop, calls=%fused_computation.32 | loop fusion | flops 1022 | bytes 2064 | tf_op jit(solution)/shard_map/reduce_sum | solution.py:55
  47.4 21.9 %all-reduce.3 = (f32[]{:T(128)}, f32[]{:T(128)}) all-reduce(f32[]{:T(128)} %get-tuple-element.227, f32[]{:T(128)} %get-tuple-element.226), channel_id=1, replica_groups=mesh['grp'=4,'mem'=8] {'mem'}, use_global_device_ids=true, to_apply=%region_3.0 | all-reduce | flops 2 | bytes 16 | tf_op jit(solution)/shard_map/psum | solution.py:54
  69.3 6.6 %all-reduce.4 = (f32[]{:T(128)}, f32[]{:T(128)}) all-reduce(f32[]{:T(128)} %get-tuple-element.217, f32[]{:T(128)} %get-tuple-element.218), channel_id=1, replica_groups=mesh['grp'=4,'mem'=8] {'grp'}, use_global_device_ids=true, to_apply=%region_4.0 | all-reduce | flops 2 | bytes 16 | tf_op jit(solution)/shard_map/psum | solution.py:53
  77.2 0.8 pad_maximum_fusion.1
  78.1 31.4 %all_gather.7 = f32[65,2048]{1,0:T(8,128)S(1)} all-gather(f32[65,256]{1,0:T(8,128)S(1)} %pad_maximum_fusion.1), channel_id=1, replica_groups=mesh['grp'=4,'mem'=8] {'mem'}, dimensions={1}, use_global_device_ids=true | all-gather | bytes 599040 | tf_op jit(solution)/shard_map/all_gather | solution.py:72
  109.5 0.7 copy-done
  111.6 5.9 %all_gather.6 = f32[65,1024]{1,0:T(8,128)S(1)} all-gather(f32[65,256]{1,0:T(8,128)S(1)} %pad_maximum_fusion), channel_id=1, replica_groups=mesh['grp'=4,'mem'=8] {'grp'}, dimensions={1}, use_global_device_ids=true | all-gather | bytes 332800 | tf_op jit(solution)/shard_map/all_gather | solution.py:73
  117.5 0.7 slice-done
  118.2 18.0 %while.20 = (s32[]{:T(128)}, f32[2048]{0:T(1024)S(1)}, f32[2048]{0:T(1024)S(1)}, f32[1024]{0:T(1024)S(1)}, f32[1024]{0:T(1024)S(1)}, /*index=5*/f32[65,1024]{1,0...) while((s32[]{:T(128)}, f32[2048]{0:T(1024)S(1)}, ...), condition=%wide.region_17.0_spmd.clone, body=%wide.region_11.0_spmd.clone.sunk | while | flops 204761344 | bytes 2844898 | solution.py:48
  118.2 1.3 subtract_reduce_fusion.3
  120.4 1.3 subtract_reduce_fusion.3
  122.7 1.3 subtract_reduce_fusion.3
  125.0 1.3 subtract_reduce_fusion.3
  127.2 1.3 subtract_reduce_fusion.3
  129.5 1.3 subtract_reduce_fusion.3
  131.7 1.3 subtract_reduce_fusion.3
  134.0 1.3 subtract_reduce_fusion.3
  136.2 6.2 %pmax.31 = f32[1024]{0:T(1024)S(1)} all-reduce(f32[1024]{0:T(1024)S(1)} %get-tuple-element.161), channel_id=1, replica_groups=mesh['grp'=4,'mem'=8] {'grp'}, use_global_device_ids=true, to_apply=%region_20.0 | all-reduce | flops 1024 | bytes 8192 | tf_op jit(solution)/shard_map/pmax | solution.py:93
  142.4 5.7 %all-reduce.1 = f32[1024]{0:T(1024)S(1)} all-reduce(f32[1024]{0:T(1024)S(1)} %exponential_multiply_fusion.1), channel_id=3, replica_groups=mesh['grp'=4,'mem'=8] {'grp'}, use_global_device_ids=true, to_apply=%region_21.0.clone | all-reduce | flops 1024 | bytes 8192
  150.6 17.5 %pmax.30 = f32[2048]{0:T(1024)S(1)} all-reduce(f32[2048]{0:T(1024)S(1)} %get-tuple-element.159), channel_id=1, replica_groups=mesh['grp'=4,'mem'=8] {'mem'}, use_global_device_ids=true, to_apply=%region_18.0 | all-reduce | flops 2048 | bytes 16384 | tf_op jit(solution)/shard_map/pmax | solution.py:87
  168.1 19.3 %all-reduce = f32[2048]{0:T(1024)S(1)} all-reduce(f32[2048]{0:T(1024)S(1)} %exponential_multiply_fusion), channel_id=2, replica_groups=mesh['grp'=4,'mem'=8] {'mem'}, use_global_device_ids=true, to_apply=%region_19.0.clone | all-reduce | flops 2048 | bytes 16384
  (119 shorter events, 11.5 us)
Async XLA Ops:
  0.6 1.3 copy-start.2
  44.7 0.7 copy-start.3
  76.6 0.7 copy-start.5
  109.5 0.8 copy-start
  109.5 2.1 %copy-start.1 = (f32[64,256]{1,0:T(8,128)S(1)}, f32[64,256]{1,0:T(8,128)}, u32[]{:S(2)}) copy-start(f32[64,256]{1,0:T(8,128)} %param.9) | copy-start | bytes 196612
  110.9 0.7 copy-start.4
  117.5 0.7 slice-start
  148.1 0.7 copy-start.7
  187.4 0.7 copy-start.6

commit v2 on v0

--- a/solution.py
+++ b/solution.py
@@ -66,7 +66,9 @@
     col_term = target_logw - tgt_norm + target_pot / epsilon
     moving = jnp.concatenate([target_pts, col_term[None, :]], 0)
     standing = jnp.concatenate([source_pts, row_term[None, :]], 0)
-    row_block = lax.all_gather(standing, "mem", axis=1, tiled=True)
+    row_block = jnp.concatenate(
+        lax.all_to_all(jnp.stack([standing] * lax.axis_size("mem")), "mem", 0, 0), axis=1
+    )
     col_block = lax.all_gather(moving, "grp", axis=1, tiled=True)
     block_pts = row_block[:-1]
     block_terms = row_block[-1]

time: 206 us -> 181 us (0.88)
  blocking collectives: 172 us -> 137 us
  starting transfers between devices: 0 us -> 5.52 us
  waiting for transfers between devices: 0 us -> 4.84 us
    all_gather x1 -> x0, blocking collectives: 31.4 us -> none  [local(): row_block = lax.all_gather(standing, 'mem', axis=1, tiled=True)]
    all_to_all x0 -> x1, starting transfers between devices: none -> 5.52 us  [local(): lax.all_to_all(jnp.stack([standing] * lax.axis_size('mem')), 'mem', 0, 0)]
    all_to_all x0 -> x1, waiting for transfers between devices: none -> 4.84 us  [local(): lax.all_to_all(jnp.stack([standing] * lax.axis_size('mem')), 'mem', 0, 0)]
  transfers between devices with their start and end apart: 0 -> 1, of which waited for: 0 -> 1; matrix products, arithmetic and copies ran while one was open for 0% -> 1% of each run, Pallas kernels for 0% -> 0%
where the time goes in v2:
time: 181 us; the launch traced here: 180 us
  blocking collectives  137 us (76%)
  other arithmetic  13 us (7%)
  matrix products  10.5 us (6%)
  starting transfers between devices  5.52 us (3%)
  waiting for transfers between devices  4.84 us (3%)
  between operations  4.62 us (3%)
  local copies, waits for them, and re-layouts  3.58 us (2%)
    pmax x1, blocking collectives, totals(): lax.pmax((jnp.max(source_logw), jnp.max(target_logw)), ('grp', 'mem'))  42.2 us
    psum x1, blocking collectives, totals(): lax.psum((jnp.sum(jnp.exp(source_logw - peaks[0])), jnp.sum(jnp.exp(targe...  40.5 us
    unnamed x2, blocking collectives  23.4 us
    pmax x1, blocking collectives, local(): rpeak = lax.pmax(row_max, 'mem')  19.5 us
    dot_general x8, matrix products, block(): lax.dot_general(points, ycols, (((0,), (0,)), ((), ())), precision=lax.Pr...  10.5 us
    all_gather x1, blocking collectives, local(): col_block = lax.all_gather(moving, 'grp', axis=1, tiled=True)  5.94 us
    pmax x1, blocking collectives, local(): cpeak = lax.pmax(col_max, 'grp')  5.67 us
    all_to_all x1, starting transfers between devices, local(): lax.all_to_all(jnp.stack([standing] * lax.axis_size('mem')), 'mem', 0, 0)  5.52 us
  transfers between devices with their start and end apart: 1, of which 1 were waited for; matrix products, arithmetic and copies ran while one was open for 1% of the time, Pallas kernels for 0%

profile of v2, /device:TPU:0, one launch (start us, length us, event | category | flops | bytes accessed | tf_op | source)
XLA Modules:
  0.0 179.9 jit_solution(13230917379900003433)
XLA Ops:
  0.6 1.3 reduce_max.44
  2.5 42.2 %all-reduce.3 = (f32[]{:T(128)}, f32[]{:T(128)}) all-reduce(f32[]{:T(128)} %reduce_max.44, f32[]{:T(128)} %reduce_max.45), channel_id=1, replica_groups=mesh['grp'=4,'mem'=8] {'grp','mem'}, use_global_device_ids=true, to_apply=%region_1.0 | all-reduce | flops 2 | bytes 16 | tf_op jit(solution)/shard_map/pmax | solution.py:52
  44.7 0.7 copy-done.2
  45.4 2.0 %exponential_reduce_fusion.2 = (f32[]{:T(128)}, f32[]{:T(128)}) fusion(f32[256]{0:T(256)S(1)} %copy-done.1, f32[]{:T(128)} %get-tuple-element.218, f32[256]{0:T(256)S(1)} %copy-done.2, f32[]{:T(128)} %get-tuple-element.217), kind=kLoop, calls=%fused_computation.33 | loop fusion | flops 1022 | bytes 2064 | tf_op jit(solution)/shard_map/reduce_sum | solution.py:54
  47.4 40.5 %all-reduce.2 = (f32[]{:T(128)}, f32[]{:T(128)}) all-reduce(f32[]{:T(128)} %get-tuple-element.225, f32[]{:T(128)} %get-tuple-element.224), channel_id=1, replica_groups=mesh['grp'=4,'mem'=8] {'grp','mem'}, use_global_device_ids=true, to_apply=%region_3.0 | all-reduce | flops 2 | bytes 16 | tf_op jit(solution)/shard_map/psum | solution.py:53
  89.3 0.8 pad_maximum_fusion.1
  90.2 0.8 stack.2
  91.0 5.5 %all-to-all-start = ((f32[8,65,256]{2,1,0:T(8,128)}), f32[8,65,256]{2,1,0:T(8,128)S(1)}, u32[]{:S(2)}, u32[]{:S(2)}) async-start(f32[8,65,256]{2,1,0:T(8,128)} %stack.2), calls=%async_computation | async-start | bytes 1179648 | tf_op jit(solution)/shard_map/all_to_all | solution.py:70
  100.2 0.7 copy-done.3
  100.9 5.9 %all_gather.3 = f32[65,1024]{1,0:T(8,128)S(1)} all-gather(f32[65,256]{1,0:T(8,128)S(1)} %pad_maximum_fusion), channel_id=1, replica_groups=mesh['grp'=4,'mem'=8] {'grp'}, dimensions={1}, use_global_device_ids=true | all-gather | bytes 332800 | tf_op jit(solution)/shard_map/all_gather | solution.py:72
  106.9 4.8 %all-to-all-done = f32[8,65,256]{2,1,0:T(8,128)S(1)} async-done(((f32[8,65,256]{2,1,0:T(8,128)}), f32[8,65,256]{2,1,0:T(8,128)S(1)}, u32[]{:S(2)}, u32[]{:S(2)}) %all-to-all-start) | async-done | bytes 532512 | tf_op jit(solution)/shard_map/all_to_all | solution.py:70
  111.9 18.1 %while.20 = (s32[]{:T(128)}, f32[2048]{0:T(1024)S(1)}, f32[2048]{0:T(1024)S(1)}, f32[1024]{0:T(1024)S(1)}, f32[1024]{0:T(1024)S(1)}, /*index=5*/f32[65,1024]{1,0...) while((s32[]{:T(128)}, f32[2048]{0:T(1024)S(1)}, ...), condition=%wide.region_15.0_spmd.clone, body=%wide.region_9.0_spmd.clone.sunk | while | flops 204761344 | bytes 2844898 | solution.py:48
  112.0 1.3 subtract_reduce_fusion.3
  114.2 1.3 subtract_reduce_fusion.3
  116.5 1.3 subtract_reduce_fusion.3
  118.7 1.3 subtract_reduce_fusion.3
  121.0 1.3 subtract_reduce_fusion.3
  123.3 1.3 subtract_reduce_fusion.3
  125.5 1.3 subtract_reduce_fusion.3
  127.8 1.3 subtract_reduce_fusion.3
  130.0 5.7 %pmax.31 = f32[1024]{0:T(1024)S(1)} all-reduce(f32[1024]{0:T(1024)S(1)} %get-tuple-element.161), channel_id=1, replica_groups=mesh['grp'=4,'mem'=8] {'grp'}, use_global_device_ids=true, to_apply=%region_18.0 | all-reduce | flops 1024 | bytes 8192 | tf_op jit(solution)/shard_map/pmax | solution.py:92
  135.7 6.0 %all-reduce.1 = f32[1024]{0:T(1024)S(1)} all-reduce(f32[1024]{0:T(1024)S(1)} %exponential_multiply_fusion.1), channel_id=3, replica_groups=mesh['grp'=4,'mem'=8] {'grp'}, use_global_device_ids=true, to_apply=%region_19.0.clone | all-reduce | flops 1024 | bytes 8192
  141.7 19.5 %pmax.30 = f32[2048]{0:T(1024)S(1)} all-reduce(f32[2048]{0:T(1024)S(1)} %get-tuple-element.159), channel_id=1, replica_groups=mesh['grp'=4,'mem'=8] {'mem'}, use_global_device_ids=true, to_apply=%region_16.0 | all-reduce | flops 2048 | bytes 16384 | tf_op jit(solution)/shard_map/pmax | solution.py:86
  161.2 17.4 %all-reduce = f32[2048]{0:T(1024)S(1)} all-reduce(f32[2048]{0:T(1024)S(1)} %exponential_multiply_fusion), channel_id=2, replica_groups=mesh['grp'=4,'mem'=8] {'mem'}, use_global_device_ids=true, to_apply=%region_17.0.clone | all-reduce | flops 2048 | bytes 16384
  (119 shorter events, 10.3 us)
Async XLA Ops:
  0.6 1.3 copy-start.1
  44.7 0.7 copy-start.2
  88.6 0.7 copy-start.4
  91.0 6.8 %copy-start.6 = (u32[32]{0:T(128)S(1)}, u32[32]{0:T(128)}, u32[]{:S(2)}) copy-start(u32[32]{0:T(128)} %constant.93) | copy-start | bytes 388
  91.0 7.4 %copy-start.5 = (u32[32]{0:T(128)S(1)}, u32[32]{0:T(128)}, u32[]{:S(2)}) copy-start(u32[32]{0:T(128)} %constant.89) | copy-start | bytes 388
  91.0 20.7 %all-to-all-start = ((f32[8,65,256]{2,1,0:T(8,128)}), f32[8,65,256]{2,1,0:T(8,128)S(1)}, u32[]{:S(2)}, u32[]{:S(2)}) async-start(f32[8,65,256]{2,1,0:T(8,128)} %stack.2), calls=%async_computation | async-start | bytes 1179648 | tf_op jit(solution)/shard_map/all_to_all | solution.py:70
  96.5 4.4 %copy-start = (f32[64,256]{1,0:T(8,128)S(1)}, f32[64,256]{1,0:T(8,128)}, u32[]{:S(2)}) copy-start(f32[64,256]{1,0:T(8,128)} %param.9) | copy-start | bytes 196612
  100.2 0.7 copy-start.3
